TPU v7x, 32 devices: a whole 2x2x4 slice. The times are simulated.
32 devices in a mesh: wide: 4 (over y, x), narrow: 8 (over z, core).
Axes of the slice: x: 2, y: 2, z: 4, core: 2. Of those that a mesh axis runs over, the one named last changes fastest.
Arguments:
- mixture: bfloat16 [4, 64, 256, 256], P(None, ('wide', 'narrow')), may hold values from -30 to 30
- w_attn: bfloat16 [2, 4, 256, 256], replicated, may hold values from -2.625 to 2.625
- w_up: bfloat16 [2, 256, 1024], replicated, may hold values from -0.375 to 0.375
- w_down: bfloat16 [2, 1024, 256], replicated, may hold values from -0.1875 to 0.1875
- norm_gain: float32 [2, 2, 256], replicated, may hold values from 0.1 to 1.9
- norm_bias: float32 [2, 2, 256], replicated, may hold values from -3 to 3
- group_gain: float32 [2, 256], replicated, may hold values from 0.1 to 1.9
- group_bias: float32 [2, 256], replicated, may hold values from -3 to 3
Outputs:
- separated: bfloat16 [4, 64, 256, 256], P(None, ('wide', 'narrow'))
All inputs are finite; a program needn't handle non-finite values.
Results may differ from a plain program's by a relative error of at most 0.0083.
Values may be sent and summed in bfloat16 or wider, within the bound.
A program may use at most 64 MiB of HBM per device.

v0:
```python
import math

import jax
import jax.numpy as jnp
from jax import lax
from jax.sharding import PartitionSpec as P

HEADS = 8


EPSILON = 1e-05


def positions_table(seq_length, model_width):
    positions = jnp.arange(seq_length, dtype=jnp.float32)[:, None]
    freq_index = jnp.arange(model_width // 2, dtype=jnp.float32)[None, :]
    angles = positions * jnp.exp(freq_index * (-2.0 * math.log(10000.0) / model_width))
    return jnp.concatenate([jnp.sin(angles), jnp.cos(angles)], axis=1)


def layer_norm(values, gain_row, bias_row):
    mean_value = jnp.mean(values, axis=-1, keepdims=True)
    centered = values - mean_value
    variance = jnp.mean(centered * centered, axis=-1, keepdims=True)
    return centered * lax.rsqrt(variance + EPSILON) * gain_row + bias_row


def encoder_block(seq_block, pos_table, attn_weights, up_weight, down_weight, gains, biases):
    groups, seq_length, inner_count, model_width = seq_block.shape
    head_size = model_width // HEADS
    state_rows = seq_block.astype(jnp.float32) + pos_table[None, :, None, :]
    normed = (
        layer_norm(state_rows, gains[0], biases[0]).astype(jnp.bfloat16).reshape(-1, model_width)
    )

    def project(matrix):
        product = jnp.dot(normed, matrix, preferred_element_type=jnp.float32).astype(jnp.bfloat16)
        return product.reshape(groups, seq_length, inner_count, HEADS, head_size)

    queries = project(attn_weights[0])
    key_rows = project(attn_weights[1])
    value_rows = project(attn_weights[2])
    scores = jnp.einsum("alnhe,amnhe->anhlm", queries, key_rows, preferred_element_type=jnp.float32)
    scores = scores * (1.0 / math.sqrt(head_size))
    shifted = jnp.exp(scores - jnp.max(scores, axis=-1, keepdims=True))
    weights = (shifted / jnp.sum(shifted, axis=-1, keepdims=True)).astype(jnp.bfloat16)
    attended = jnp.einsum(
        "anhlm,amnhe->alnhe", weights, value_rows, preferred_element_type=jnp.float32
    )
    attended = attended.astype(jnp.bfloat16).reshape(-1, model_width)
    mixed = jnp.dot(attended, attn_weights[3], preferred_element_type=jnp.float32)
    state_after = state_rows + mixed.reshape(state_rows.shape)
    normed_two = (
        layer_norm(state_after, gains[1], biases[1]).astype(jnp.bfloat16).reshape(-1, model_width)
    )
    hidden = jax.nn.relu(jnp.dot(normed_two, up_weight, preferred_element_type=jnp.float32)).astype(
        jnp.bfloat16
    )
    output = jnp.dot(hidden, down_weight, preferred_element_type=jnp.float32)
    return state_after + output.reshape(state_after.shape)


def run_layer(seq_data, layer_index, w_attn, w_up, w_down, norm_gain, norm_bias, block_rows):
    seq_count, seq_length, inner_count, model_width = seq_data.shape
    per_block = math.gcd(seq_count, max(1, block_rows // (seq_length * inner_count)))
    pos_table = positions_table(seq_length, model_width)
    blocked = seq_data.reshape(
        seq_count // per_block, per_block, seq_length, inner_count, model_width
    )

    def apply_block(seq_block):
        return encoder_block(
            seq_block,
            pos_table,
            w_attn[layer_index],
            w_up[layer_index],
            w_down[layer_index],
            norm_gain[layer_index],
            norm_bias[layer_index],
        )

    return lax.map(apply_block, blocked).reshape(seq_count, seq_length, inner_count, model_width)


def group_norm(values, gain_row, bias_row):
    cell_count = (
        values.shape[1] * lax.axis_size(("wide", "narrow")) * values.shape[2] * values.shape[3]
    )
    totals, squares = lax.psum(
        (jnp.sum(values, axis=(1, 2, 3)), jnp.sum(values * values, axis=(1, 2, 3))),
        ("wide", "narrow"),
    )
    mean_flat = totals / cell_count
    variance = squares / cell_count - mean_flat * mean_flat
    centered = values - mean_flat[:, None, None, None]
    return centered * lax.rsqrt(variance[:, None, None, None] + EPSILON) * gain_row + bias_row


def on_device(mixture, w_attn, w_up, w_down, norm_gain, norm_bias, group_gain, group_bias):
    mix_count, segs_here, frame_count, model_width = mixture.shape
    intra_out = run_layer(
        mixture.reshape(mix_count * segs_here, frame_count, 1, model_width),
        0,
        w_attn,
        w_up,
        w_down,
        norm_gain,
        norm_bias,
        512,
    ).reshape(mixture.shape)
    carried = (
        group_norm(intra_out, group_gain[0], group_bias[0]) + mixture.astype(jnp.float32)
    ).astype(jnp.bfloat16)
    result = run_layer(
        lax.all_to_all(carried, ("wide", "narrow"), split_axis=2, concat_axis=1, tiled=True),
        1,
        w_attn,
        w_up,
        w_down,
        norm_gain,
        norm_bias,
        512,
    ).astype(jnp.bfloat16)
    inter_out = lax.all_to_all(result, ("wide", "narrow"), split_axis=1, concat_axis=2, tiled=True)
    separated = group_norm(
        inter_out.astype(jnp.float32), group_gain[1], group_bias[1]
    ) + carried.astype(jnp.float32)
    return separated.astype(jnp.bfloat16)


def solution(mesh):
    in_specs = (P(None, ("wide", "narrow"), None, None), P(), P(), P(), P(), P(), P(), P())
    out_specs = P(None, ("wide", "narrow"), None, None)
    return jax.shard_map(
        on_device, mesh=mesh, in_specs=in_specs, out_specs=out_specs, check_vma=False
    )
```

profile of v0, /device:TPU:0, one launch (start us, length us, event | category | flops | bytes accessed | tf_op | source)
XLA Modules:
  0.0 287.9 jit_solution(8594341458941040517)
XLA Ops:
  0.5 69.5 %while.20 = (s32[]{:T(128)}, f32[4,2,256,1,256]{4,2,1,3,0:T(8,128)S(1)}, bf16[4,2,256,1,256]{4,2,1,3,0:T(8,128)(2,1)}, f32[256,256]{1,0:T(8,128)S(1)}, f32[2,2,2...) while((s32[]{:T(128)}, ...), condition=%wide.region_7.8_spmd, body=%wide.region_0.7_spmd.sunk | while | flops 950011136 | bytes 32064172 | solution.py:82
  1.7 1.2 fusion.220
  3.7 1.2 fusion.221
  4.8 1.1 convolution_convert_fusion.14
  7.5 3.5 %fusion.222 = (f32[2,8,256]{2,1,0:T(8,128)S(1)}, f32[2,8,256,256]{2,3,1,0:T(8,128)}) fusion(bf16[2,256,8,32]{1,0,3,2:T(2,128)(2,1)S(1)} %reshape.950, bf16[2,256,8,32]{1,0,3,2:T(2,128)(2,1)S(1)} %reshape.951), kind=kOutput, calls=%fused_computation.148.clone.1 | convolution fusion | flops 70254848 | bytes 4734976 | tf_op jit(solution)/shard_map/while/body/eval_jaxpr/sub | solution.py:45
  11.0 1.1 convolution_convert_fusion.16
  12.4 2.6 fusion.223
  15.0 1.5 fusion.224
  19.1 1.2 fusion.220
  21.1 1.2 fusion.221
  23.6 1.1 convolution_convert_fusion.15
  24.9 3.4 %fusion.222 = (f32[2,8,256]{2,1,0:T(8,128)S(1)}, f32[2,8,256,256]{2,3,1,0:T(8,128)}) fusion(bf16[2,256,8,32]{1,0,3,2:T(2,128)(2,1)S(1)} %reshape.950, bf16[2,256,8,32]{1,0,3,2:T(2,128)(2,1)S(1)} %reshape.951), kind=kOutput, calls=%fused_computation.148.clone.1 | convolution fusion | flops 70254848 | bytes 4734976 | tf_op jit(solution)/shard_map/while/body/eval_jaxpr/sub | solution.py:45
  29.7 2.6 fusion.223
  32.4 1.5 fusion.224
  36.4 1.2 fusion.220
  38.4 1.2 fusion.221
  42.3 3.4 %fusion.222 = (f32[2,8,256]{2,1,0:T(8,128)S(1)}, f32[2,8,256,256]{2,3,1,0:T(8,128)}) fusion(bf16[2,256,8,32]{1,0,3,2:T(2,128)(2,1)S(1)} %reshape.950, bf16[2,256,8,32]{1,0,3,2:T(2,128)(2,1)S(1)} %reshape.951), kind=kOutput, calls=%fused_computation.148.clone.1 | convolution fusion | flops 70254848 | bytes 4734976 | tf_op jit(solution)/shard_map/while/body/eval_jaxpr/sub | solution.py:45
  47.1 2.6 fusion.223
  49.7 1.5 fusion.224
  53.8 1.2 fusion.220
  55.8 1.2 fusion.221
  59.7 3.4 %fusion.222 = (f32[2,8,256]{2,1,0:T(8,128)S(1)}, f32[2,8,256,256]{2,3,1,0:T(8,128)}) fusion(bf16[2,256,8,32]{1,0,3,2:T(2,128)(2,1)S(1)} %reshape.950, bf16[2,256,8,32]{1,0,3,2:T(2,128)(2,1)S(1)} %reshape.951), kind=kOutput, calls=%fused_computation.148.clone.1 | convolution fusion | flops 70254848 | bytes 4734976 | tf_op jit(solution)/shard_map/while/body/eval_jaxpr/sub | solution.py:45
  64.5 2.6 fusion.223
  67.1 1.5 fusion.224
  71.8 41.9 %all-reduce.1 = (f32[4]{0:T(128)S(1)}, f32[4]{0:T(128)S(1)}) all-reduce(f32[4]{0:T(128)S(1)} %fusion.124, f32[4]{0:T(128)S(1)} %reduce_sum.126), channel_id=1, replica_groups=mesh['wide'=4,'narrow'=8] {'wide','narrow'}, use_global_device_ids=true, to_apply=%region_11.12 | all-reduce | flops 8 | bytes 64 | tf_op jit(solution)/shard_map/psum | solution.py:89
  115.3 1.8 copy.87
  117.1 4.6 %all-to-all-start = ((bf16[4,2,256,256]{3,0,1,2:T(4,128)(2,1)}), bf16[4,2,256,256]{3,0,1,2:T(4,128)(2,1)S(1)}, u32[]{:S(2)}, u32[]{:S(2)}) async-start(bf16[4,2,256,256]{3,0,1,2:T(4,128)(2,1)} %copy.87), calls=%async_computation | async-start | bytes 2097152 | tf_op jit(solution)/shard_map/all_to_all | solution.py:115
  121.9 27.1 %all-to-all-done = bf16[4,2,256,256]{3,0,1,2:T(4,128)(2,1)S(1)} async-done(((bf16[4,2,256,256]{3,0,1,2:T(4,128)(2,1)}), bf16[4,2,256,256]{3,0,1,2:T(4,128)(2,1)S(1)}, u32[]{:S(2)}, u32[]{:S(2)}) %all-to-all-start) | async-done | bytes 1048608 | tf_op jit(solution)/shard_map/all_to_all | solution.py:115
  149.2 69.6 %while.21 = (s32[]{:T(128)}, bf16[4,1,64,8,256]{4,3,0,2,1:T(8,128)(2,1)}, bf16[4,1,64,8,256]{4,3,2,1,0:T(8,128)(2,1)S(1)}, f32[64,256]{1,0:T(8,128)S(1)}, f32[2,...) while((s32[]{:T(128)}, ...), condition=%wide.region_19.20_spmd, body=%wide.region_12.19_spmd.sunk | while | flops 864556160 | bytes 17468152 | solution.py:82
  149.7 1.2 convolution_convert_fusion.18
  151.4 1.2 convolution_convert_fusion.19
  153.1 2.7 fusion.246
  155.7 2.0 fusion.245
  157.7 1.2 convolution_convert_fusion.17
  159.4 2.7 convolution_convert_fusion.20
  162.4 1.3 fusion.247
  164.0 2.6 fusion.248
  167.1 1.2 convolution_convert_fusion.18
  168.8 1.2 convolution_convert_fusion.19
  170.4 2.7 fusion.246
  173.1 2.0 fusion.245
  175.1 1.2 convolution_convert_fusion.17
  176.8 2.7 convolution_convert_fusion.20
  179.8 1.3 fusion.247
  181.4 2.6 fusion.248
  184.5 1.2 convolution_convert_fusion.18
  186.2 1.2 convolution_convert_fusion.19
  187.8 2.7 fusion.246
  190.5 2.0 fusion.245
  192.5 1.2 convolution_convert_fusion.17
  194.2 2.7 convolution_convert_fusion.20
  197.2 1.3 fusion.247
  198.8 2.6 fusion.248
  201.8 1.2 convolution_convert_fusion.18
  203.5 1.2 convolution_convert_fusion.19
  205.2 2.7 fusion.246
  207.9 2.0 fusion.245
  209.9 1.2 convolution_convert_fusion.17
  211.6 2.7 convolution_convert_fusion.20
  214.6 1.3 fusion.247
  216.1 2.6 fusion.248
  218.8 30.2 %all_to_all.24 = bf16[4,64,8,256]{3,2,0,1:T(8,128)(2,1)S(1)} all-to-all(bf16[4,64,8,256]{3,2,0,1:T(8,128)(2,1)} %bitcast.314), channel_id=1, replica_groups=mesh['wide'=4,'narrow'=8] {'wide','narrow'}, dimensions={1} | all-to-all | bytes 2097152 | tf_op jit(solution)/shard_map/all_to_all | solution.py:124
  249.5 36.8 %all-reduce = (f32[4]{0:T(128)S(1)}, f32[4]{0:T(128)S(1)}) all-reduce(f32[4]{0:T(128)S(1)} %get-tuple-element.102, f32[4]{0:T(128)S(1)} %get-tuple-element.101), channel_id=1, replica_groups=mesh['wide'=4,'narrow'=8] {'wide','narrow'}, use_global_device_ids=true, to_apply=%region_23.24 | all-reduce | flops 8 | bytes 64 | tf_op jit(solution)/shard_map/psum | solution.py:89
  286.3 1.6 fusion.118
  (211 shorter events, 39.2 us)
Async XLA Ops:
  15.0 2.1 copy-start.15
  15.0 2.5 copy-start.3
  32.3 2.1 copy-start.15
  32.3 2.5 copy-start.3
  49.7 2.1 copy-start.15
  49.7 2.5 copy-start.3
  67.1 2.1 copy-start.15
  67.1 2.5 copy-start.3
  70.0 0.7 copy-start.13
  70.1 1.2 copy-start.14
  70.1 43.7 %copy-start = (bf16[4,2,256,1,256]{4,2,1,3,0:T(8,128)(2,1)S(1)}, bf16[4,2,256,1,256]{4,2,1,3,0:T(8,128)(2,1)}, u32[]{:S(2)}) copy-start(bf16[4,2,256,1,256]{4,2,1,3,0:T(8,128)(2,1)} %get-tuple-element.371) | copy-start | bytes 3145732
  114.3 1.0 copy-start.1
  117.1 32.1 %copy-start.5 = (f32[2,2,256]{2,1,0:T(2,128)S(1)}, f32[2,2,256]{2,1,0:T(2,128)}, u32[]{:S(2)}) copy-start(f32[2,2,256]{2,1,0:T(2,128)} %get-tuple-element.375) | copy-start | bytes 12292
  117.1 32.1 %copy-start.6 = (f32[2,2,256]{2,1,0:T(2,128)S(1)}, f32[2,2,256]{2,1,0:T(2,128)}, u32[]{:S(2)}) copy-start(f32[2,2,256]{2,1,0:T(2,128)} %get-tuple-element.376) | copy-start | bytes 12292
  117.1 31.9 %all-to-all-start = ((bf16[4,2,256,256]{3,0,1,2:T(4,128)(2,1)}), bf16[4,2,256,256]{3,0,1,2:T(4,128)(2,1)S(1)}, u32[]{:S(2)}, u32[]{:S(2)}) async-start(bf16[4,2,256,256]{3,0,1,2:T(4,128)(2,1)} %copy.87), calls=%async_computation | async-start | bytes 2097152 | tf_op jit(solution)/shard_map/all_to_all | solution.py:115
  149.7 1.7 copy-start.7
  149.7 1.7 copy-start.9
  155.7 2.0 copy-start.8
  155.7 2.0 copy-start.10
  162.2 1.8 copy-start.4
  167.0 1.7 copy-start.7
  167.0 1.7 copy-start.9
  173.1 2.0 copy-start.8
  173.1 2.0 copy-start.10
  179.5 1.8 copy-start.4
  184.4 1.7 copy-start.7
  184.5 1.7 copy-start.9
  190.5 2.0 copy-start.8
  190.5 2.0 copy-start.10
  197.0 1.8 copy-start.4
  201.8 1.7 copy-start.7
  201.8 1.7 copy-start.9
  207.9 2.0 copy-start.8
  207.9 2.0 copy-start.10
  214.3 1.8 copy-start.4
  218.8 67.5 %copy-start.2 = (bf16[4,2,256,256]{3,2,1,0:T(8,128)(2,1)S(1)}, bf16[4,2,256,256]{3,2,1,0:T(8,128)(2,1)}, u32[]{:S(2)}) copy-start(bf16[4,2,256,256]{3,2,1,0:T(8,128)(2,1)} %copy-done.1) | copy-start | bytes 3145732
  218.8 67.5 %copy-start.11 = (f32[1,256]{1,0:T(1,128)S(1)}, f32[1,256]{1,0:T(1,128)}, u32[]{:S(2)}) copy-start(f32[1,256]{1,0:T(1,128)} %get-tuple-element.161) | copy-start | bytes 3076
  218.8 67.5 %copy-start.12 = (f32[1,256]{1,0:T(1,128)S(1)}, f32[1,256]{1,0:T(1,128)}, u32[]{:S(2)}) copy-start(f32[1,256]{1,0:T(1,128)} %get-tuple-element.163) | copy-start | bytes 3076
where the time goes:
time: 290 us; the launch traced here: 288 us
  blocking collectives  109 us (38%)
  matrix products  107 us (37%)
  waiting for transfers between devices  27.1 us (9%)
  other arithmetic  22.1 us (8%)
  local copies, waits for them, and re-layouts  16.2 us (6%)
  starting transfers between devices  4.58 us (2%)
    psum x2, blocking collectives, group_norm(): lax.psum((jnp.sum(values, axis=(1, 2, 3)), jnp.sum(values * values, axis=...  78.7 us
    all_to_all x1, blocking collectives, on_device(): lax.all_to_all(result, ('wide', 'narrow'), split_axis=1, concat_axis=2, t...  30.2 us
    dot_general x24, matrix products, project(): jnp.dot(normed, matrix, preferred_element_type=jnp.float32)  28.3 us
    all_to_all x1, waiting for transfers between devices, on_device(): lax.all_to_all(carried, ('wide', 'narrow'), split_axis=2, concat_axis=1,...  27.1 us
    sub x8, matrix products, encoder_block(): shifted = jnp.exp(scores - jnp.max(scores, axis=-1, keepdims=True))  21.7 us
    dot_general x8, matrix products, encoder_block(): jnp.einsum('anhlm,amnhe->alnhe', weights, value_rows, preferred_element_t...  21.4 us
    dot_general x8, matrix products, encoder_block(): output = jnp.dot(hidden, down_weight, preferred_element_type=jnp.float32)  12.3 us
    dot_general x8, matrix products, encoder_block(): jnp.dot(attended, attn_weights[3], preferred_element_type=jnp.float32)  11.1 us
  transfers between devices with their start and end apart: 1, of which 1 were waited for; matrix products, arithmetic and copies ran while one was open for 0% of the time, Pallas kernels for 0%

commit v1 on v0

--- a/solution.py
+++ b/solution.py
@@ -1,11 +1,15 @@
+import functools
 import math
 
 import jax
 import jax.numpy as jnp
 from jax import lax
+from jax.experimental import pallas as pl
+from jax.experimental.pallas import tpu as pltpu
 from jax.sharding import PartitionSpec as P
 
 HEADS = 8
+MESH = pl.DeviceIdType.MESH
 
 
 EPSILON = 1e-05
@@ -128,9 +132,355 @@
     return separated.astype(jnp.bfloat16)
 
 
+def pick_sizes(mixture, device_count):
+    _, segs_here, frame_count, model_width = mixture.shape
+    seq_length = segs_here * device_count
+    frames_here = frame_count // device_count
+    group_rows = min(frame_count, seq_length * frames_here)
+    fits = (
+        frames_here == 8
+        and frame_count % 128 == 0
+        and 128 % seq_length == 0
+        and group_rows % 128 == 0
+        and (seq_length * frames_here) % group_rows == 0
+        and model_width % 128 == 0
+        and 128 % (model_width // HEADS) == 0
+    )
+    return fits, seq_length, frames_here, group_rows
+
+
+def dot(left, right, left_dim=1, right_dim=0):
+    return lax.dot_general(
+        left, right, (((left_dim,), (right_dim,)), ((), ())), preferred_element_type=jnp.float32
+    )
+
+
+def group_layer(state_rows, seq_length, attn, up_weight, down_weight, gains, biases):
+    rows, model_width = state_rows.shape
+    head_size = model_width // HEADS
+    heads_in_tile = 128 // head_size
+    scale = math.log2(math.e) / math.sqrt(head_size)
+    normed = layer_norm(state_rows, gains[0:1], biases[0:1]).astype(jnp.bfloat16)
+    queries = dot(attn(0), normed, 1, 1).astype(jnp.bfloat16)
+    key_rows = dot(normed, attn(1)).astype(jnp.bfloat16)
+    value_cols = dot(attn(2), normed, 1, 1).astype(jnp.bfloat16)
+    zero_rows = jnp.zeros((head_size, rows), jnp.bfloat16)
+    packed = seq_length < rows
+    if packed:
+        lane_seq = lax.broadcasted_iota(jnp.int32, (seq_length, 128), 1) // seq_length
+        seqs_in_tile = 128 // seq_length
+    parts = []
+    for head in range(HEADS):
+        tile, place = divmod(head, heads_in_tile)
+        own = queries[head * head_size : (head + 1) * head_size]
+        spread = jnp.concatenate(
+            [own if i == place else zero_rows for i in range(heads_in_tile)], axis=0
+        )
+        scores = dot(key_rows[:, tile * 128 : (tile + 1) * 128], spread)
+        if packed:
+            columns = []
+            for lane_tile in range(rows // 128):
+                block = None
+                for i in range(seqs_in_tile):
+                    first = (lane_tile * seqs_in_tile + i) * seq_length
+                    piece = scores[
+                        first : first + seq_length, lane_tile * 128 : (lane_tile + 1) * 128
+                    ]
+                    block = piece if block is None else jnp.where(lane_seq == i, piece, block)
+                columns.append(block)
+            scores = jnp.concatenate(columns, axis=1)
+        shifted = jnp.exp2((scores - jnp.max(scores, axis=0, keepdims=True)) * scale)
+        inverse = 1.0 / jnp.sum(shifted, axis=0, keepdims=True)
+        if packed:
+            row_blocks = []
+            for seq in range(rows // seq_length):
+                lane_tile, i = divmod(seq, seqs_in_tile)
+                kept = jnp.where(
+                    lane_seq == i, shifted[:, lane_tile * 128 : (lane_tile + 1) * 128], 0.0
+                )
+                none = jnp.zeros_like(kept)
+                row_blocks.append(
+                    jnp.concatenate(
+                        [kept if t == lane_tile else none for t in range(rows // 128)], axis=1
+                    )
+                )
+            shifted = jnp.concatenate(row_blocks, axis=0)
+        attended = dot(
+            value_cols[head * head_size : (head + 1) * head_size], shifted.astype(jnp.bfloat16)
+        )
+        parts.append((attended * inverse).astype(jnp.bfloat16))
+    mixed = dot(jnp.concatenate(parts, axis=0), attn(3), 0, 0)
+    state_after = state_rows + mixed
+    normed_two = layer_norm(state_after, gains[1:2], biases[1:2]).astype(jnp.bfloat16)
+    hidden = jnp.maximum(dot(normed_two, up_weight), 0.0).astype(jnp.bfloat16)
+    return state_after + dot(hidden, down_weight)
+
+
+def lane_sums(values):
+    column = jnp.sum(values, axis=0, keepdims=True)
+    total = column[:, 0:128]
+    for tile in range(1, values.shape[1] // 128):
+        total = total + column[:, tile * 128 : (tile + 1) * 128]
+    return total
+
+
+def fused_kernel(
+    axis_names,
+    axis_sizes,
+    seq_length,
+    frames_here,
+    group_rows,
+    x_ref,
+    attn_ref,
+    up_ref,
+    down_ref,
+    ngain_ref,
+    nbias_ref,
+    ggain_ref,
+    gbias_ref,
+    pos0_ref,
+    pos1_ref,
+    out_ref,
+    y_scr,
+    carried_scr,
+    recv_scr,
+    inter_scr,
+    back_scr,
+    rows_scr,
+    stat_scr,
+    send_sem,
+    recv_sem,
+):
+    mixes, segs_here, frame_count, model_width = x_ref.shape
+    n = axis_sizes[0] * axis_sizes[1]
+    me = lax.axis_index(axis_names[0]) * axis_sizes[1] + lax.axis_index(axis_names[1])
+    cells = float(n * segs_here * frame_count * model_width)
+    lane_tiles = model_width // 128
+
+    def device_of(index):
+        return (index // axis_sizes[1], lax.rem(index, axis_sizes[1]))
+
+    barrier = pltpu.get_barrier_semaphore()
+
+    def greet(k, carry):
+        pl.semaphore_signal(
+            barrier, inc=1, device_id=device_of(lax.rem(me + k, n)), device_id_type=MESH
+        )
+        return carry
+
+    lax.fori_loop(1, n, greet, 0)
+
+    def send_all(kind, b, source, target):
+        def send(k, carry):
+            peer = lax.rem(me + k, n)
+            pltpu.make_async_remote_copy(
+                src_ref=source(peer),
+                dst_ref=target(),
+                send_sem=send_sem.at[kind, b],
+                recv_sem=recv_sem.at[kind, b],
+                device_id=device_of(peer),
+                device_id_type=MESH,
+            ).start()
+            return carry
+
+        lax.fori_loop(1, n, send, 0)
+
+    def arrived(ref, sem):
+        pltpu.make_async_copy(ref, ref, sem).wait()
+
+    def stat_block(which, b):
+        return stat_scr.at[which, b, pl.ds(0, n - 1)]
+
+    def share_stats(which, b, sums, squares):
+        stat_scr[which, b, me, 0:1, :] = sums
+        stat_scr[which, b, me, 1:2, :] = squares
+        send_all(
+            which,
+            b,
+            lambda peer: stat_scr.at[which, b, me],
+            lambda: stat_scr.at[which, b, me],
+        )
+
+    def affine(which, b):
+        arrived(stat_block(which, b), recv_sem.at[which, b])
+        total = jnp.sum(stat_scr[which, b], axis=0)
+        flat = jnp.sum(total, axis=1, keepdims=True) / cells
+        mean = flat[0:1]
+        variance = flat[1:2] - mean * mean
+        gain = lax.rsqrt(variance + EPSILON) * ggain_ref[which : which + 1]
+        return gain, gbias_ref[which : which + 1] - mean * gain
+
+    def weights(layer):
+        return (
+            lambda i: attn_ref[layer, i],
+            up_ref[layer],
+            down_ref[layer],
+            ngain_ref[layer],
+            nbias_ref[layer],
+        )
+
+    def intra(b):
+        def one(c, sums):
+            state = x_ref[b, c].astype(jnp.float32) + pos0_ref[...]
+            y = group_layer(state, frame_count, *weights(0))
+            y_scr[b, c] = y
+            return sums[0] + lane_sums(y), sums[1] + lane_sums(y * y)
+
+        zero = jnp.zeros((1, 128), jnp.float32)
+        return lax.fori_loop(0, segs_here, one, (zero, zero))
+
+    def carry_out(b):
+        gain, bias = affine(0, b)
+
+        def one(c, carry):
+            full = y_scr[b, c] * gain + bias + x_ref[b, c].astype(jnp.float32)
+            carried_scr[b, c] = full.reshape(n, frames_here, model_width).astype(jnp.bfloat16)
+            return carry
+
+        lax.fori_loop(0, segs_here, one, 0)
+        recv_scr[b, pl.ds(me * segs_here, segs_here)] = carried_scr[b, :, me]
+        send_all(
+            2,
+            b,
+            lambda peer: carried_scr.at[b, :, peer],
+            lambda: recv_scr.at[b, pl.ds(me * segs_here, segs_here)],
+        )
+
+    def first_half(step, carry):
+        @pl.when(step < mixes)
+        def _():
+            sums, squares = intra(step)
+
+            @pl.when(step == 0)
+            def _():
+                pl.semaphore_wait(barrier, n - 1)
+
+            share_stats(0, step, sums, squares)
+
+        @pl.when(step >= 1)
+        def _():
+            carry_out(step - 1)
+
+        return carry
+
+    lax.fori_loop(0, mixes + 1, first_half, 0)
+
+    seqs = group_rows // seq_length
+
+    def inter(b, carry):
+        arrived(recv_scr.at[b, pl.ds(0, (n - 1) * segs_here)], recv_sem.at[2, b])
+        wide_rows = recv_scr[b].astype(jnp.float32).reshape(seq_length * frames_here, model_width)
+        for t in range(lane_tiles):
+            rows_scr[t] = wide_rows[:, t * 128 : (t + 1) * 128]
+
+        def one(g, sums):
+            blocks = []
+            for i in range(seqs):
+                picked = [
+                    rows_scr[t, pl.ds(g * seqs + i, seq_length, stride=frames_here), :]
+                    for t in range(lane_tiles)
+                ]
+                blocks.append(jnp.concatenate(picked, axis=1) + pos1_ref[...])
+            y = group_layer(jnp.concatenate(blocks, axis=0), seq_length, *weights(1))
+            y = y.astype(jnp.bfloat16).astype(jnp.float32)
+            for i in range(seqs):
+                for t in range(lane_tiles):
+                    rows_scr[t, pl.ds(g * seqs + i, seq_length, stride=frames_here), :] = y[
+                        i * seq_length : (i + 1) * seq_length, t * 128 : (t + 1) * 128
+                    ]
+            return sums[0] + lane_sums(y), sums[1] + lane_sums(y * y)
+
+        zero = jnp.zeros((1, 128), jnp.float32)
+        sums, squares = lax.fori_loop(0, frames_here // seqs, one, (zero, zero))
+        for t in range(lane_tiles):
+            inter_scr[b, :, :, t * 128 : (t + 1) * 128] = (
+                rows_scr[t].reshape(seq_length, frames_here, 128).astype(jnp.bfloat16)
+            )
+        back_scr[b, :, me] = inter_scr[b, pl.ds(me * segs_here, segs_here)]
+        share_stats(1, b, sums, squares)
+        send_all(
+            3,
+            b,
+            lambda peer: inter_scr.at[b, pl.ds(peer * segs_here, segs_here)],
+            lambda: back_scr.at[b, :, me],
+        )
+        return carry
+
+    lax.fori_loop(0, mixes, inter, 0)
+
+    def finish(b, carry):
+        gain, bias = affine(1, b)
+        arrived(back_scr.at[b, :, pl.ds(0, n - 1)], recv_sem.at[3, b])
+
+        def one(c, inner):
+            full = back_scr[b, c].astype(jnp.float32) * gain + bias
+            full = full + carried_scr[b, c].astype(jnp.float32)
+            out_ref[b, c] = full.reshape(frame_count, model_width).astype(jnp.bfloat16)
+            return inner
+
+        lax.fori_loop(0, segs_here, one, 0)
+        arrived(stat_block(0, b), send_sem.at[0, b])
+        arrived(stat_block(1, b), send_sem.at[1, b])
+        arrived(carried_scr.at[b, :, pl.ds(0, n - 1)], send_sem.at[2, b])
+        arrived(inter_scr.at[b, pl.ds(0, (n - 1) * segs_here)], send_sem.at[3, b])
+        return carry
+
+    lax.fori_loop(0, mixes, finish, 0)
+
+
+def fused(mesh, mixture, w_attn, w_up, w_down, norm_gain, norm_bias, group_gain, group_bias):
+    axis_names = ("wide", "narrow")
+    axis_sizes = tuple(mesh.shape[name] for name in axis_names)
+    n = axis_sizes[0] * axis_sizes[1]
+    mixes, segs_here, frame_count, model_width = mixture.shape
+    _, seq_length, frames_here, group_rows = pick_sizes(mixture, n)
+    turned = jnp.swapaxes(w_attn, 2, 3)
+    attn = jnp.stack([turned[:, 0], w_attn[:, 1], turned[:, 2], w_attn[:, 3]], axis=1)
+    split = (mixes, segs_here, n, frames_here, model_width)
+    joined = (mixes, seq_length, frames_here, model_width)
+    return pl.pallas_call(
+        functools.partial(
+            fused_kernel, axis_names, axis_sizes, seq_length, frames_here, group_rows
+        ),
+        out_shape=jax.ShapeDtypeStruct(mixture.shape, jnp.bfloat16),
+        in_specs=[pl.BlockSpec(memory_space=pltpu.VMEM)] * 10,
+        out_specs=pl.BlockSpec(memory_space=pltpu.VMEM),
+        scratch_shapes=[
+            pltpu.VMEM(mixture.shape, jnp.float32),
+            pltpu.VMEM(split, jnp.bfloat16),
+            pltpu.VMEM(joined, jnp.bfloat16),
+            pltpu.VMEM(joined, jnp.bfloat16),
+            pltpu.VMEM(split, jnp.bfloat16),
+            pltpu.VMEM((model_width // 128, seq_length * frames_here, 128), jnp.float32),
+            pltpu.VMEM((2, mixes, n, 2, 128), jnp.float32),
+            pltpu.SemaphoreType.DMA((4, mixes)),
+            pltpu.SemaphoreType.DMA((4, mixes)),
+        ],
+        compiler_params=pltpu.CompilerParams(
+            collective_id=0, has_side_effects=True, vmem_limit_bytes=60 * 1024 * 1024
+        ),
+    )(
+        mixture,
+        attn,
+        w_up,
+        w_down,
+        norm_gain,
+        norm_bias,
+        group_gain,
+        group_bias,
+        positions_table(frame_count, model_width),
+        positions_table(seq_length, model_width),
+    )
+
+
 def solution(mesh):
     in_specs = (P(None, ("wide", "narrow"), None, None), P(), P(), P(), P(), P(), P(), P())
     out_specs = P(None, ("wide", "narrow"), None, None)
-    return jax.shard_map(
-        on_device, mesh=mesh, in_specs=in_specs, out_specs=out_specs, check_vma=False
-    )
+
+    def step(mixture, *parameters):
+        device_count = mesh.shape["wide"] * mesh.shape["narrow"]
+        if pick_sizes(mixture, device_count)[0]:
+            return fused(mesh, mixture, *parameters)
+        return on_device(mixture, *parameters)
+
+    return jax.shard_map(step, mesh=mesh, in_specs=in_specs, out_specs=out_specs, check_vma=False)

time: 290 us -> 89.9 us (0.31)
  blocking collectives: 109 us -> 0 us
  matrix products: 107 us -> 0 us
  Pallas kernels: 0 us -> 82.7 us
  waiting for transfers between devices: 27.1 us -> 0 us
  other arithmetic: 22.1 us -> 3.1 us
  local copies, waits for them, and re-layouts: 16.2 us -> 3.9 us
  starting transfers between devices: 4.58 us -> 0 us
    dot_general x56 -> x0, matrix products: 85.6 us -> none  [the longest x24 28.3 us: project(): jnp.dot(normed, matrix, preferred_element_type=jnp.float32)]
    pallas_call x0 -> x1, Pallas kernels: none -> 82.7 us  [fused(): pl.pallas_call(functools.partial(fused_kernel, axis_names, axis_sizes, se...]
    psum x2 -> x0, blocking collectives: 78.7 us -> none  [group_norm(): lax.psum((jnp.sum(values, axis=(1, 2, 3)), jnp.sum(values * values, axis=...]
    all_to_all x1 -> x0, blocking collectives: 30.2 us -> none  [on_device(): lax.all_to_all(result, ('wide', 'narrow'), split_axis=1, concat_axis=2, t...]
    all_to_all x1 -> x0, waiting for transfers between devices: 27.1 us -> none  [on_device(): lax.all_to_all(carried, ('wide', 'narrow'), split_axis=2, concat_axis=1,...]
    sub x8 -> x0, matrix products: 21.7 us -> none  [encoder_block(): shifted = jnp.exp(scores - jnp.max(scores, axis=-1, keepdims=True))]
    reduce_sum x27 -> x0, other arithmetic: 13.6 us -> none  [the longest x16 7.6 us: layer_norm(): variance = jnp.mean(centered * centered, axis=-1, keepdims=True)]
    convert_element_type x10 -> x0, other arithmetic: 7.55 us -> none  [the longest x4 4.61 us: encoder_block(): layer_norm(state_rows, gains[0], biases[0]).astype(jnp.bfloat16)]
  transfers between devices with their start and end apart: 1 -> 0, of which waited for: 1 -> 0; matrix products, arithmetic and copies ran while one was open for 0% -> 0% of each run, Pallas kernels for 0% -> 0%
where the time goes in v1:
time: 89.9 us; the launch traced here: 89.7 us
  Pallas kernels  82.7 us (92%)
  local copies, waits for them, and re-layouts  3.9 us (4%)
  other arithmetic  3.1 us (3%)
    pallas_call x1, Pallas kernels, fused(): pl.pallas_call(functools.partial(fused_kernel, axis_names, axis_sizes, se...  82.7 us
    unnamed x4, local copies, waits for them, and re-layouts  3.83 us

profile of v1, /device:TPU:0, one launch (start us, length us, event | category | flops | bytes accessed | tf_op | source)
XLA Modules:
  0.0 89.7 jit_solution(11302043442496604052)
XLA Ops:
  0.0 0.0 copy-start
  0.0 1.6 %copy.9 = bf16[2,4,256,256]{2,3,1,0:T(8,128)(2,1)S(1)} copy(bf16[2,4,256,256]{3,2,1,0:T(8,128)(2,1)} %param.9) | data formatting | bytes 2097152 | tf_op args[1]
  1.6 0.0 copy-done
  1.6 0.1 fusion.4
  1.7 1.1 %pad_maximum_fusion.attn_ref = bf16[2,4,256,256]{3,2,1,0:T(8,128)(2,1)} fusion(bf16[2,1,256,256]{3,2,1,0:T(8,128)(2,1)S(1)} %get-tuple-element.13, bf16[2,1,256,256]{3,2,1,0:T(8,128)(2,1)S(1)} %get-tuple-element.6, bf16[2,1,256,256]{3,2,1,0:T(8,128)(2,1)S(1)} %get-tuple-element.14, bf16[2,1,256,256]{3,2,1,0:T(8,128)(2,1)S(1)} %get-tuple-element.5), kind=kLoop, calls=%fused_computation | loop fusion | flops 1572864 | bytes 2097152 | tf_op jit(solution)/shard_map/stack | solution.py:438
  2.8 0.5 fusion.1
  3.3 0.7 pad_maximum_fusion.1.pos0_ref
  4.0 0.1 fusion.3
  4.1 0.6 pad_maximum_fusion.2.pos1_ref
  4.8 82.7 %shard_map.82 = bf16[4,2,256,256]{3,2,1,0:T(8,128)(2,1)} custom-call(bf16[4,2,256,256]{3,2,1,0:T(8,128)(2,1)} %x_ref.1, bf16[2,4,256,256]{3,2,1,0:T(8,128)(2,1)} %pad_maximum_fusion.attn_ref, bf16[2,256,1024]{2,1,0:T(8,128)(2,1)} %up_ref.1, bf16[2,1024,256]{2,1,0:T(8,128)(2,1)} %down_ref.1, f32[2,2,256]{2,1,0:T(2,128)} %ngain_ref.1, f32[2,2,256]{2,1,0:T(2,128)} %nbias_ref.1, ...), custom_call_target="tpu_custom_call" | custom-call | tf_op jit(solution)/shard_map/pallas_call | solution.py:441
  87.5 2.3 %copy.11 = bf16[4,2,256,256]{3,2,1,0:T(8,128)(2,1)} copy(bf16[4,2,256,256]{3,2,1,0:T(8,128)(2,1)} %shard_map.82) | data formatting | bytes 2097152
  (1 shorter events, 0.0 us)
Async XLA Ops:
  0.0 1.6 %copy-start = (bf16[2,4,256,256]{3,2,1,0:T(8,128)(2,1)S(1)}, bf16[2,4,256,256]{3,2,1,0:T(8,128)(2,1)}, u32[]{:S(2)}) copy-start(bf16[2,4,256,256]{3,2,1,0:T(8,128)(2,1)} %param.9) | copy-start | bytes 3145732

commit v2 on v1

--- a/solution.py
+++ b/solution.py
@@ -3,6 +3,7 @@
 
 import jax
 import jax.numpy as jnp
+import numpy as np
 from jax import lax
 from jax.experimental import pallas as pl
 from jax.experimental.pallas import tpu as pltpu
@@ -132,6 +133,13 @@
     return separated.astype(jnp.bfloat16)
 
 
+def fixed_positions(seq_length, model_width):
+    positions = np.arange(seq_length, dtype=np.float64)[:, None]
+    freq_index = np.arange(model_width // 2, dtype=np.float64)[None, :]
+    angles = positions * np.exp(freq_index * (-2.0 * math.log(10000.0) / model_width))
+    return np.concatenate([np.sin(angles), np.cos(angles)], axis=1).astype(np.float32)
+
+
 def pick_sizes(mixture, device_count):
     _, segs_here, frame_count, model_width = mixture.shape
     seq_length = segs_here * device_count
@@ -161,22 +169,37 @@
     heads_in_tile = 128 // head_size
     scale = math.log2(math.e) / math.sqrt(head_size)
     normed = layer_norm(state_rows, gains[0:1], biases[0:1]).astype(jnp.bfloat16)
-    queries = dot(attn(0), normed, 1, 1).astype(jnp.bfloat16)
+    queries = (dot(attn(0), normed, 1, 1) * scale).astype(jnp.bfloat16)
     key_rows = dot(normed, attn(1)).astype(jnp.bfloat16)
     value_cols = dot(attn(2), normed, 1, 1).astype(jnp.bfloat16)
     zero_rows = jnp.zeros((head_size, rows), jnp.bfloat16)
+    one_rows = jnp.ones((16, rows), jnp.bfloat16)
     packed = seq_length < rows
     if packed:
         lane_seq = lax.broadcasted_iota(jnp.int32, (seq_length, 128), 1) // seq_length
         seqs_in_tile = 128 // seq_length
     parts = []
-    for head in range(HEADS):
+
+    def score(head):
         tile, place = divmod(head, heads_in_tile)
         own = queries[head * head_size : (head + 1) * head_size]
         spread = jnp.concatenate(
             [own if i == place else zero_rows for i in range(heads_in_tile)], axis=0
         )
-        scores = dot(key_rows[:, tile * 128 : (tile + 1) * 128], spread)
+        return dot(key_rows[:, tile * 128 : (tile + 1) * 128], spread)
+
+    def attend(head):
+        own_values = value_cols[head * head_size : (head + 1) * head_size]
+        attended = dot(jnp.concatenate([own_values, one_rows], axis=0), waiting[head])
+        inverse = 1.0 / attended[head_size : head_size + 1]
+        return (attended[:head_size] * inverse).astype(jnp.bfloat16)
+
+    waiting = []
+    ahead = [score(0), score(1)]
+    for head in range(HEADS):
+        scores = ahead[head]
+        if head + 2 < HEADS:
+            ahead.append(score(head + 2))
         if packed:
             columns = []
             for lane_tile in range(rows // 128):
@@ -189,8 +212,7 @@
                     block = piece if block is None else jnp.where(lane_seq == i, piece, block)
                 columns.append(block)
             scores = jnp.concatenate(columns, axis=1)
-        shifted = jnp.exp2((scores - jnp.max(scores, axis=0, keepdims=True)) * scale)
-        inverse = 1.0 / jnp.sum(shifted, axis=0, keepdims=True)
+        shifted = jnp.exp2(scores - jnp.max(scores, axis=0, keepdims=True))
         if packed:
             row_blocks = []
             for seq in range(rows // seq_length):
@@ -205,10 +227,10 @@
                     )
                 )
             shifted = jnp.concatenate(row_blocks, axis=0)
-        attended = dot(
-            value_cols[head * head_size : (head + 1) * head_size], shifted.astype(jnp.bfloat16)
-        )
-        parts.append((attended * inverse).astype(jnp.bfloat16))
+        waiting.append(shifted.astype(jnp.bfloat16))
+        if head >= 1:
+            parts.append(attend(head - 1))
+    parts.append(attend(HEADS - 1))
     mixed = dot(jnp.concatenate(parts, axis=0), attn(3), 0, 0)
     state_after = state_rows + mixed
     normed_two = layer_norm(state_after, gains[1:2], biases[1:2]).astype(jnp.bfloat16)
@@ -248,6 +270,7 @@
     back_scr,
     rows_scr,
     stat_scr,
+    turned_scr,
     send_sem,
     recv_sem,
 ):
@@ -269,6 +292,10 @@
         return carry
 
     lax.fori_loop(1, n, greet, 0)
+
+    for layer in range(2):
+        for i in range(2):
+            turned_scr[layer, i] = attn_ref[layer, 2 * i].T
 
     def send_all(kind, b, source, target):
         def send(k, carry):
@@ -312,7 +339,7 @@
 
     def weights(layer):
         return (
-            lambda i: attn_ref[layer, i],
+            lambda i: turned_scr[layer, i // 2] if i % 2 == 0 else attn_ref[layer, i],
             up_ref[layer],
             down_ref[layer],
             ngain_ref[layer],
@@ -327,7 +354,7 @@
             return sums[0] + lane_sums(y), sums[1] + lane_sums(y * y)
 
         zero = jnp.zeros((1, 128), jnp.float32)
-        return lax.fori_loop(0, segs_here, one, (zero, zero))
+        return lax.fori_loop(0, segs_here, one, (zero, zero), unroll=True)
 
     def carry_out(b):
         gain, bias = affine(0, b)
@@ -391,7 +418,7 @@
             return sums[0] + lane_sums(y), sums[1] + lane_sums(y * y)
 
         zero = jnp.zeros((1, 128), jnp.float32)
-        sums, squares = lax.fori_loop(0, frames_here // seqs, one, (zero, zero))
+        sums, squares = lax.fori_loop(0, frames_here // seqs, one, (zero, zero), unroll=True)
         for t in range(lane_tiles):
             inter_scr[b, :, :, t * 128 : (t + 1) * 128] = (
                 rows_scr[t].reshape(seq_length, frames_here, 128).astype(jnp.bfloat16)
@@ -434,8 +461,6 @@
     n = axis_sizes[0] * axis_sizes[1]
     mixes, segs_here, frame_count, model_width = mixture.shape
     _, seq_length, frames_here, group_rows = pick_sizes(mixture, n)
-    turned = jnp.swapaxes(w_attn, 2, 3)
-    attn = jnp.stack([turned[:, 0], w_attn[:, 1], turned[:, 2], w_attn[:, 3]], axis=1)
     split = (mixes, segs_here, n, frames_here, model_width)
     joined = (mixes, seq_length, frames_here, model_width)
     return pl.pallas_call(
@@ -453,6 +478,7 @@
             pltpu.VMEM(split, jnp.bfloat16),
             pltpu.VMEM((model_width // 128, seq_length * frames_here, 128), jnp.float32),
             pltpu.VMEM((2, mixes, n, 2, 128), jnp.float32),
+            pltpu.VMEM((2, 2, model_width, model_width), jnp.bfloat16),
             pltpu.SemaphoreType.DMA((4, mixes)),
             pltpu.SemaphoreType.DMA((4, mixes)),
         ],
@@ -461,15 +487,15 @@
         ),
     )(
         mixture,
-        attn,
+        w_attn,
         w_up,
         w_down,
         norm_gain,
         norm_bias,
         group_gain,
         group_bias,
-        positions_table(frame_count, model_width),
-        positions_table(seq_length, model_width),
+        jnp.asarray(fixed_positions(frame_count, model_width)),
+        jnp.asarray(fixed_positions(seq_length, model_width)),
     )
 
 

time: 89.9 us -> 70.6 us (0.79)
  Pallas kernels: 82.7 us -> 68.1 us
  other arithmetic: 3.1 us -> 0 us
  local copies, waits for them, and re-layouts: 3.9 us -> 2.26 us
    pallas_call x1, Pallas kernels: 82.7 us -> 68.1 us  [fused(): pl.pallas_call(functools.partial(fused_kernel, axis_names, axis_sizes, se...]
    unnamed x4 -> x1, local copies, waits for them, and re-layouts: 3.83 us -> 2.26 us
    concatenate x2 -> x0, other arithmetic: 1.34 us -> none  [positions_table(): return jnp.concatenate([jnp.sin(angles), jnp.cos(angles)], axis=1)]
    another operation x1 -> x0, other arithmetic: 1.1 us -> none  [fused(): jnp.stack([turned[:, 0], w_attn[:, 1], turned[:, 2], w_attn[:, 3]], axis=1)]
where the time goes in v2:
time: 70.6 us; the launch traced here: 70.4 us
  Pallas kernels  68.1 us (96%)
  local copies, waits for them, and re-layouts  2.26 us (3%)
    pallas_call x1, Pallas kernels, fused(): pl.pallas_call(functools.partial(fused_kernel, axis_names, axis_sizes, se...  68.1 us
    unnamed x1, local copies, waits for them, and re-layouts  2.26 us

profile of v2, /device:TPU:0, one launch (start us, length us, event | category | flops | bytes accessed | tf_op | source)
XLA Modules:
  0.0 70.4 jit_solution(10986568114135993817)
XLA Ops:
  0.0 68.1 %shard_map.100 = bf16[4,2,256,256]{3,2,1,0:T(8,128)(2,1)} custom-call(bf16[4,2,256,256]{3,2,1,0:T(8,128)(2,1)} %x_ref.1, bf16[2,4,256,256]{3,2,1,0:T(8,128)(2,1)} %attn_ref.1, bf16[2,256,1024]{2,1,0:T(8,128)(2,1)} %up_ref.1, bf16[2,1024,256]{2,1,0:T(8,128)(2,1)} %down_ref.1, f32[2,2,256]{2,1,0:T(2,128)} %ngain_ref.1, f32[2,2,256]{2,1,0:T(2,128)} %nbias_ref.1, ...), custom_call_target="tpu_custom_call" | custom-call | tf_op jit(solution)/shard_map/pallas_call | solution.py:466
  68.2 2.3 %copy.12 = bf16[4,2,256,256]{3,2,1,0:T(8,128)(2,1)} copy(bf16[4,2,256,256]{3,2,1,0:T(8,128)(2,1)} %shard_map.100) | data formatting | bytes 2097152

commit v3 on v2

--- a/solution.py
+++ b/solution.py
@@ -291,7 +291,7 @@
         )
         return carry
 
-    lax.fori_loop(1, n, greet, 0)
+    lax.fori_loop(1, n, greet, 0, unroll=True)
 
     for layer in range(2):
         for i in range(2):
@@ -310,7 +310,7 @@
             ).start()
             return carry
 
-        lax.fori_loop(1, n, send, 0)
+        lax.fori_loop(1, n, send, 0, unroll=True)
 
     def arrived(ref, sem):
         pltpu.make_async_copy(ref, ref, sem).wait()

time: 70.6 us -> 69.8 us (0.989)
  Pallas kernels: 68.1 us -> 67.3 us
    pallas_call x1, Pallas kernels: 68.1 us -> 67.3 us  [fused(): pl.pallas_call(functools.partial(fused_kernel, axis_names, axis_sizes, se...]
where the time goes in v3:
time: 69.8 us; the launch traced here: 69.6 us
  Pallas kernels  67.3 us (96%)
  local copies, waits for them, and re-layouts  2.26 us (3%)
    pallas_call x1, Pallas kernels, fused(): pl.pallas_call(functools.partial(fused_kernel, axis_names, axis_sizes, se...  67.3 us
    unnamed x1, local copies, waits for them, and re-layouts  2.26 us

profile of v3, /device:TPU:0, one launch (start us, length us, event | category | flops | bytes accessed | tf_op | source)
XLA Modules:
  0.0 69.6 jit_solution(9486931900396927351)
XLA Ops:
  0.0 67.3 %shard_map.100 = bf16[4,2,256,256]{3,2,1,0:T(8,128)(2,1)} custom-call(bf16[4,2,256,256]{3,2,1,0:T(8,128)(2,1)} %x_ref.1, bf16[2,4,256,256]{3,2,1,0:T(8,128)(2,1)} %attn_ref.1, bf16[2,256,1024]{2,1,0:T(8,128)(2,1)} %up_ref.1, bf16[2,1024,256]{2,1,0:T(8,128)(2,1)} %down_ref.1, f32[2,2,256]{2,1,0:T(2,128)} %ngain_ref.1, f32[2,2,256]{2,1,0:T(2,128)} %nbias_ref.1, ...), custom_call_target="tpu_custom_call" | custom-call | tf_op jit(solution)/shard_map/pallas_call | solution.py:466
  67.3 2.3 %copy.12 = bf16[4,2,256,256]{3,2,1,0:T(8,128)(2,1)} copy(bf16[4,2,256,256]{3,2,1,0:T(8,128)(2,1)} %shard_map.100) | data formatting | bytes 2097152
